TPU v7x, 32 devices: a whole 2x2x4 slice. The times are simulated.
32 devices in a mesh: expert: 4 (over y, core), unit: 8 (over z, x).
Axes of the slice: x: 2, y: 2, z: 4, core: 2. Of those that a mesh axis runs over, the one named last changes fastest.
Arguments:
- a_gate: bfloat16 [4, 14336, 4096], P('expert', 'unit'), may hold values from -0.09375 to 0.09375
- a_up: bfloat16 [4, 14336, 4096], P('expert', 'unit'), may hold values from -0.09375 to 0.09375
- b_gate: bfloat16 [4, 14336, 4096], P('expert', 'unit'), may hold values from -0.09375 to 0.09375
- b_up: bfloat16 [4, 14336, 4096], P('expert', 'unit'), may hold values from -0.09375 to 0.09375
- order: int32 [4, 448], P('expert'), may hold values from 0 to 447, each once within a row
- calib: bfloat16 [128, 4096], P(('expert', 'unit')), may hold values from -6 to 6
Outputs:
- merged_gate: bfloat16 [4, 14336, 4096], P('expert', 'unit')
- merged_up: bfloat16 [4, 14336, 4096], P('expert', 'unit')
- hidden: bfloat16 [4, 14336, 128], P('expert', 'unit')
Inputs may be any that keep to these rules, and one draw needn't show every extreme that they name: Each row of order is a permutation of the 448 block numbers.
All inputs are finite; a program needn't handle non-finite values.
Results may differ from a plain program's by a relative error of at most 0.006.
Values may be sent and summed in bfloat16 or wider, within the bound.
A program may use at most 256 MiB of HBM per device.

v0:
```python
import jax
import jax.numpy as jnp
from jax import lax
from jax.sharding import PartitionSpec as P

BLOCK = 32


def average(first, second):
    return ((first.astype(jnp.float32) + second.astype(jnp.float32)) * 0.5).astype(jnp.bfloat16)


def local(a_gate, a_up, b_gate, b_up, order, calib):
    blocks = order.shape[1]
    total = blocks * BLOCK
    inverse = jnp.zeros((blocks,), jnp.int32).at[order[0]].set(jnp.arange(blocks, dtype=jnp.int32))

    def relocate(columns):
        grouped = columns.reshape(blocks, BLOCK, columns.shape[1])
        return jnp.take(grouped, inverse, axis=0).reshape(total, columns.shape[1])

    gathered = (
        lax.all_to_all(b_gate[0], "unit", split_axis=1, concat_axis=0, tiled=True),
        lax.all_to_all(b_up[0], "unit", split_axis=1, concat_axis=0, tiled=True),
    )
    returned = (
        lax.all_to_all(relocate(gathered[0]), "unit", split_axis=0, concat_axis=1, tiled=True),
        lax.all_to_all(relocate(gathered[1]), "unit", split_axis=0, concat_axis=1, tiled=True),
    )
    merged_gate = average(a_gate[0], returned[0])
    merged_up = average(a_up[0], returned[1])
    dims = (((1,), (1,)), ((), ()))
    piece = lax.all_gather(calib, ("expert", "unit"), axis=0, tiled=True)
    gate_pre = lax.dot_general(merged_gate, piece, dims, preferred_element_type=jnp.float32)
    up_pre = lax.dot_general(merged_up, piece, dims, preferred_element_type=jnp.float32)
    hidden = (jax.nn.silu(gate_pre) * up_pre).astype(jnp.bfloat16)
    return (merged_gate[None], merged_up[None], hidden[None])


def solution(mesh):
    in_specs = (
        P("expert", "unit", None),
        P("expert", "unit", None),
        P("expert", "unit", None),
        P("expert", "unit", None),
        P("expert", None),
        P(("expert", "unit"), None),
    )
    out_specs = (P("expert", "unit", None), P("expert", "unit", None), P("expert", "unit", None))
    return jax.shard_map(local, mesh=mesh, in_specs=in_specs, out_specs=out_specs, check_vma=False)
```

profile of v0, /device:TPU:0, one launch (start us, length us, event | category | flops | bytes accessed | tf_op | source)
XLA Modules:
  0.0 1635.2 jit_solution(6001479759196739935)
XLA Ops:
  7.2 18.6 %copy.22 = bf16[1,1792,4096]{1,2,0:T(8,128)(2,1)} copy(bf16[1,1792,4096]{2,1,0:T(8,128)(2,1)} %param.10) | data formatting | bytes 29360128 | tf_op args[2]
  33.1 18.6 %copy.26 = bf16[1,1792,4096]{1,2,0:T(8,128)(2,1)} copy(bf16[1,1792,4096]{2,1,0:T(8,128)(2,1)} %param.11) | data formatting | bytes 29360128 | tf_op args[3]
  51.7 299.4 %all-to-all-done = bf16[1792,8,512]{0,2,1:T(8,128)(2,1)} async-done(((bf16[1792,8,512]{0,2,1:T(8,128)(2,1)}), bf16[1792,8,512]{0,2,1:T(8,128)(2,1)}, u32[]{:S(2)}, u32[]{:S(2)}) %all-to-all-start) | async-done | bytes 14680096 | tf_op jit(solution)/shard_map/all_to_all | solution.py:23
  359.8 18.7 %copy.23 = bf16[8,1792,512]{2,1,0:T(8,128)(2,1)} copy(bf16[8,1792,512]{1,2,0:T(8,128)(2,1)} %bitcast.3) | data formatting | bytes 29360128 | tf_op jit(solution)/shard_map/all_to_all | solution.py:23
  378.5 295.4 %all-to-all-done.2 = bf16[1792,8,512]{0,2,1:T(8,128)(2,1)} async-done(((bf16[1792,8,512]{0,2,1:T(8,128)(2,1)}), bf16[1792,8,512]{0,2,1:T(8,128)(2,1)}, u32[]{:S(2)}, u32[]{:S(2)}) %all-to-all-start.2) | async-done | bytes 14680096 | tf_op jit(solution)/shard_map/all_to_all | solution.py:24
  673.8 18.7 %copy.27 = bf16[8,1792,512]{2,1,0:T(8,128)(2,1)} copy(bf16[8,1792,512]{1,2,0:T(8,128)(2,1)} %bitcast.9) | data formatting | bytes 29360128 | tf_op jit(solution)/shard_map/all_to_all | solution.py:24
  692.5 18.6 %gather_fusion = bf16[448,32,512]{2,1,0:T(8,128)(2,1)} fusion(bf16[448,32,512]{2,1,0:T(8,128)(2,1)} %bitcast.50, s32[1024]{0:T(1024)S(1)} %pad_clamp_fusion), kind=kCustom, calls=%fused_computation.clone | custom fusion | bytes 29361920 | tf_op jit(solution)/shard_map/jit(_take)/gather | solution.py:20
  711.1 18.6 %gather_fusion.1 = bf16[448,32,512]{2,1,0:T(8,128)(2,1)} fusion(bf16[448,32,512]{2,1,0:T(8,128)(2,1)} %bitcast.52, s32[1024]{0:T(1024)S(1)} %pad_clamp_fusion), kind=kCustom, calls=%fused_computation.1.clone | custom fusion | bytes 29361920 | tf_op jit(solution)/shard_map/jit(_take)/gather | solution.py:20
  729.7 17.3 %broadcast_select_fusion = (bf16[448,32,512]{2,1,0:T(8,128)(2,1)S(1)}, bf16[448,32,512]{2,1,0:T(8,128)(2,1)}) fusion(bf16[448,32,512]{2,1,0:T(8,128)(2,1)} %gather_fusion.1, pred[448]{0:T(512)(128)(4,1)S(1)} %compare_and_fusion, bf16[448,32,512]{2,1,0:T(8,128)(2,1)} %gather_fusion), kind=kLoop, calls=%fused_computation.19 | loop fusion | flops 14680064 | bytes 58720704 | tf_op jit(solution)/shard_map/jit(_take)/select_n | solution.py:20
  747.0 321.5 %all_to_all.58 = bf16[8,1792,512]{2,1,0:T(8,128)(2,1)} all-to-all(bf16[8,1792,512]{2,1,0:T(8,128)(2,1)S(1)} %bitcast.51), channel_id=1, replica_groups=mesh['expert'=4,'unit'=8] {'unit'}, dimensions={0} | all-to-all | bytes 29360128 | tf_op jit(solution)/shard_map/all_to_all | solution.py:28
  1074.7 18.6 %copy.21 = bf16[1,1792,4096]{1,2,0:T(8,128)(2,1)} copy(bf16[1,1792,4096]{2,1,0:T(8,128)(2,1)} %param.8) | data formatting | bytes 29360128 | tf_op args[0]
  1093.4 18.8 %copy.25 = bf16[1,1792,4096]{1,2,0:T(8,128)(2,1)} copy(bf16[1,1792,4096]{2,1,0:T(8,128)(2,1)} %param.9) | data formatting | bytes 29360128 | tf_op args[1]
  1112.1 286.1 %all-gather.3.cloned.1.call-done = bf16[32,4,4096]{2,1,0:T(4,128)(2,1)} async-done(((bf16[1,4,4096]{2,1,0:T(4,128)(2,1)}), bf16[32,4,4096]{2,1,0:T(4,128)(2,1)}) %all-gather.3.cloned.1.call-update) | async-done | bytes 1048592 | tf_op jit(solution)/shard_map/all_gather | solution.py:33
  1399.5 16.8 %convert_bitcast_fusion.2 = f32[1792,8,512]{2,0,1:T(8,128)} fusion(bf16[8,1792,512]{2,1,0:T(8,128)(2,1)} %all_to_all.58), kind=kLoop, calls=%fused_computation.17 | loop fusion | flops 7340032 | bytes 44040192 | tf_op jit(solution)/shard_map/convert_element_type | solution.py:10
  1416.3 27.6 %copy.28 = f32[1792,8,512]{0,2,1:T(8,128)} copy(f32[1792,8,512]{2,0,1:T(8,128)} %convert_bitcast_fusion.2) | data formatting | bytes 58720256 | tf_op jit(solution)/shard_map/convert_element_type | solution.py:10
  1444.0 20.5 %fusion.9 = bf16[1792,4096]{0,1:T(8,128)(2,1)} fusion(bf16[1,1792,4096]{1,2,0:T(8,128)(2,1)} %copy.25, f32[1792,8,512]{0,2,1:T(8,128)} %copy.28), kind=kLoop, calls=%fused_computation.16 | loop fusion | flops 29360128 | bytes 58720256 | tf_op jit(solution)/shard_map/convert_element_type | solution.py:10
  1471.4 14.6 fusion.6
  1486.0 16.8 %convert_bitcast_fusion.3 = f32[1792,8,512]{2,0,1:T(8,128)} fusion(bf16[8,1792,512]{2,1,0:T(8,128)(2,1)} %all-to-all-done.1), kind=kLoop, calls=%fused_computation.18 | loop fusion | flops 7340032 | bytes 44040192 | tf_op jit(solution)/shard_map/convert_element_type | solution.py:10
  1502.8 27.6 %copy.24 = f32[1792,8,512]{0,2,1:T(8,128)} copy(f32[1792,8,512]{2,0,1:T(8,128)} %convert_bitcast_fusion.3) | data formatting | bytes 58720256 | tf_op jit(solution)/shard_map/convert_element_type | solution.py:10
  1530.5 20.5 %fusion.4 = bf16[1792,4096]{0,1:T(8,128)(2,1)} fusion(bf16[1,1792,4096]{1,2,0:T(8,128)(2,1)} %copy.21, f32[1792,8,512]{0,2,1:T(8,128)} %copy.24), kind=kLoop, calls=%fused_computation.11 | loop fusion | flops 29360128 | bytes 58720256 | tf_op jit(solution)/shard_map/convert_element_type | solution.py:10
  1557.9 14.6 fusion.1
  1572.5 20.1 %copy.32 = bf16[1,1792,4096]{2,1,0:T(8,128)(2,1)} copy(bf16[1,1792,4096]{1,2,0:T(8,128)(2,1)} %fusion.6) | data formatting | bytes 29360128
  1592.6 20.1 %copy.31 = bf16[1,1792,4096]{2,1,0:T(8,128)(2,1)} copy(bf16[1,1792,4096]{1,2,0:T(8,128)(2,1)} %fusion.1) | data formatting | bytes 29360128
  1620.0 8.3 fusion.11
  (20 shorter events, 44.6 us)
Async XLA Ops:
  25.8 325.3 %all-to-all-start = ((bf16[1792,8,512]{0,2,1:T(8,128)(2,1)}), bf16[1792,8,512]{0,2,1:T(8,128)(2,1)}, u32[]{:S(2)}, u32[]{:S(2)}) async-start(bf16[1792,8,512]{0,2,1:T(8,128)(2,1)} %bitcast.48), calls=%async_computation | async-start | bytes 29360128 | tf_op jit(solution)/shard_map/all_to_all | solution.py:23
  351.1 5.7 copy-start.2
  351.1 322.8 %all-to-all-start.2 = ((bf16[1792,8,512]{0,2,1:T(8,128)(2,1)}), bf16[1792,8,512]{0,2,1:T(8,128)(2,1)}, u32[]{:S(2)}, u32[]{:S(2)}) async-start(bf16[1792,8,512]{0,2,1:T(8,128)(2,1)} %bitcast.47), calls=%async_computation.2 | async-start | bytes 29360128 | tf_op jit(solution)/shard_map/all_to_all | solution.py:24
  1068.5 417.6 %all-to-all-start.1 = ((bf16[8,1792,512]{2,1,0:T(8,128)(2,1)}), bf16[8,1792,512]{2,1,0:T(8,128)(2,1)}, u32[]{:S(2)}, u32[]{:S(2)}) async-start(bf16[8,1792,512]{2,1,0:T(8,128)(2,1)} %bitcast.49), calls=%async_computation.1 | async-start | bytes 29360128 | tf_op jit(solution)/shard_map/all_to_all | solution.py:27
  1074.0 324.2 %all-gather.3.cloned.1.call-start = ((), (), s32[]{:S(2)}) async-start(), calls=%async_computation.4 | async-start | bytes 1081344 | tf_op jit(solution)/shard_map/all_gather | solution.py:33
  1444.0 27.5 %copy-start = (f32[1792,8,512]{0,2,1:T(8,128)S(1)}, f32[1792,8,512]{0,2,1:T(8,128)}, u32[]{:S(2)}) copy-start(f32[1792,8,512]{0,2,1:T(8,128)} %copy.28) | copy-start | bytes 88080384
  1530.5 27.5 %copy-start.1 = (f32[1792,8,512]{0,2,1:T(8,128)S(1)}, f32[1792,8,512]{0,2,1:T(8,128)}, u32[]{:S(2)}) copy-start(f32[1792,8,512]{0,2,1:T(8,128)} %copy.24) | copy-start | bytes 88080384
Sparse Core Ops, SparseCore 0:
  1077.8 320.3 all-gather.2
where the time goes:
time: 1640 us
  waiting for transfers between devices  881 us (54%)
  blocking collectives  322 us (20%)
  local copies, waits for them, and re-layouts  263 us (16%)
  other arithmetic  121 us (7%)
  starting transfers between devices  18.7 us (1%)
    all_to_all x1, blocking collectives, local(): lax.all_to_all(relocate(gathered[1]), 'unit', split_axis=0, concat_axis=1...  322 us
    all_to_all x1, waiting for transfers between devices, local(): lax.all_to_all(b_gate[0], 'unit', split_axis=1, concat_axis=0, tiled=True)  299 us
    all_to_all x1, waiting for transfers between devices, local(): lax.all_to_all(b_up[0], 'unit', split_axis=1, concat_axis=0, tiled=True)  295 us
    all_gather x1, waiting for transfers between devices, local(): piece = lax.all_gather(calib, ('expert', 'unit'), axis=0, tiled=True)  286 us
    unnamed x13, local copies, waits for them, and re-layouts  130 us
    convert_element_type x4, other arithmetic, average(): ((first.astype(jnp.float32) + second.astype(jnp.float32)) * 0.5).astype(j...  70.3 us
    convert_element_type x2, local copies, waits for them, and re-layouts, average(): second.astype(jnp.float32)  55.3 us
    gather x2, local copies, waits for them, and re-layouts, relocate(): return jnp.take(grouped, inverse, axis=0).reshape(total, columns.shape[1])  37.1 us
  transfers between devices with their start and end apart: 4, of which 3 were waited for; matrix products, arithmetic and copies ran while one was open for 10% of the time, Pallas kernels for 0%

commit v1 on v0

--- a/solution.py
+++ b/solution.py
@@ -21,7 +21,12 @@
 
     gathered = (
         lax.all_to_all(b_gate[0], "unit", split_axis=1, concat_axis=0, tiled=True),
-        lax.all_to_all(b_up[0], "unit", split_axis=1, concat_axis=0, tiled=True),
+        jnp.concatenate(
+            lax.all_to_all(
+                jnp.stack(jnp.split(b_up[0], lax.axis_size("unit"), axis=1)), "unit", 0, 0
+            ),
+            axis=0,
+        ),
     )
     returned = (
         lax.all_to_all(relocate(gathered[0]), "unit", split_axis=0, concat_axis=1, tiled=True),

time: 1640 us -> 1600 us (0.976)
  waiting for transfers between devices: 881 us -> 859 us
    all_to_all x1 -> x0, local copies, waits for them, and re-layouts: 18.7 us -> none  [local(): lax.all_to_all(b_up[0], 'unit', split_axis=1, concat_axis=0, tiled=True)]
    all_to_all x1, waiting for transfers between devices: 295 us -> 277 us  [local(): lax.all_to_all(jnp.stack(jnp.split(b_up[0], lax.axis_size('unit'), axis=1...]
    unnamed x13 -> x19, local copies, waits for them, and re-layouts: 130 us -> 131 us
  transfers between devices with their start and end apart: 4 -> 4, of which waited for: 3 -> 3; matrix products, arithmetic and copies ran while one was open for 10% -> 11% of each run, Pallas kernels for 0% -> 0%
where the time goes in v1:
time: 1600 us
  waiting for transfers between devices  859 us (54%)
  blocking collectives  322 us (20%)
  local copies, waits for them, and re-layouts  248 us (16%)
  other arithmetic  121 us (8%)
  starting transfers between devices  18.6 us (1%)
    all_to_all x1, blocking collectives, local(): lax.all_to_all(relocate(gathered[1]), 'unit', split_axis=0, concat_axis=1...  322 us
    all_to_all x1, waiting for transfers between devices, local(): lax.all_to_all(b_gate[0], 'unit', split_axis=1, concat_axis=0, tiled=True)  295 us
    all_gather x1, waiting for transfers between devices, local(): piece = lax.all_gather(calib, ('expert', 'unit'), axis=0, tiled=True)  286 us
    all_to_all x1, waiting for transfers between devices, local(): lax.all_to_all(jnp.stack(jnp.split(b_up[0], lax.axis_size('unit'), axis=1...  277 us
    unnamed x19, local copies, waits for them, and re-layouts  131 us
    convert_element_type x4, other arithmetic, average(): ((first.astype(jnp.float32) + second.astype(jnp.float32)) * 0.5).astype(j...  70.3 us
    convert_element_type x2, local copies, waits for them, and re-layouts, average(): second.astype(jnp.float32)  55.3 us
    gather x2, local copies, waits for them, and re-layouts, relocate(): return jnp.take(grouped, inverse, axis=0).reshape(total, columns.shape[1])  37.1 us
  transfers between devices with their start and end apart: 4, of which 3 were waited for; matrix products, arithmetic and copies ran while one was open for 11% of the time, Pallas kernels for 0%

profile of v1, /device:TPU:0, one launch (start us, length us, event | category | flops | bytes accessed | tf_op | source)
XLA Modules:
  0.0 1597.8 jit_solution(1825311291766361249)
XLA Ops:
  7.2 18.6 %copy.20 = bf16[1,1792,4096]{1,2,0:T(8,128)(2,1)} copy(bf16[1,1792,4096]{2,1,0:T(8,128)(2,1)} %param.10) | data formatting | bytes 29360128 | tf_op args[2]
  25.8 7.3 all-to-all-start
  55.8 295.2 %all-to-all-done = bf16[1792,8,512]{0,2,1:T(8,128)(2,1)} async-done(((bf16[1792,8,512]{0,2,1:T(8,128)(2,1)}), bf16[1792,8,512]{0,2,1:T(8,128)(2,1)}, u32[]{:S(2)}, u32[]{:S(2)}) %all-to-all-start) | async-done | bytes 14680096 | tf_op jit(solution)/shard_map/all_to_all | solution.py:23
  359.6 18.7 %copy.21 = bf16[8,1792,512]{2,1,0:T(8,128)(2,1)} copy(bf16[8,1792,512]{1,2,0:T(8,128)(2,1)} %bitcast.3) | data formatting | bytes 29360128 | tf_op jit(solution)/shard_map/all_to_all | solution.py:23
  378.3 18.5 %gather_fusion = bf16[448,32,512]{2,1,0:T(8,128)(2,1)} fusion(bf16[448,32,512]{2,1,0:T(8,128)(2,1)} %bitcast.81, s32[1024]{0:T(1024)S(1)} %pad_clamp_fusion), kind=kCustom, calls=%fused_computation.clone | custom fusion | bytes 29361920 | tf_op jit(solution)/shard_map/jit(_take)/gather | solution.py:20
  396.9 276.9 %all-to-all-done.2 = bf16[8,1792,512]{2,1,0:T(8,128)(2,1)} async-done(((bf16[8,1792,512]{2,1,0:T(8,128)(2,1)}), bf16[8,1792,512]{2,1,0:T(8,128)(2,1)}, u32[]{:S(2)}, u32[]{:S(2)}) %all-to-all-start.2) | async-done | bytes 14680096 | tf_op jit(solution)/shard_map/all_to_all | solution.py:25
  673.7 18.6 %gather_fusion.1 = bf16[448,32,512]{2,1,0:T(8,128)(2,1)} fusion(bf16[448,32,512]{2,1,0:T(8,128)(2,1)} %bitcast.17, s32[1024]{0:T(1024)S(1)} %pad_clamp_fusion), kind=kCustom, calls=%fused_computation.1.clone | custom fusion | bytes 29361920 | tf_op jit(solution)/shard_map/jit(_take)/gather | solution.py:20
  692.3 17.3 %broadcast_select_fusion = (bf16[448,32,512]{2,1,0:T(8,128)(2,1)S(1)}, bf16[448,32,512]{2,1,0:T(8,128)(2,1)}) fusion(bf16[448,32,512]{2,1,0:T(8,128)(2,1)} %gather_fusion.1, pred[448]{0:T(512)(128)(4,1)S(1)} %compare_and_fusion, bf16[448,32,512]{2,1,0:T(8,128)(2,1)} %gather_fusion), kind=kLoop, calls=%fused_computation.19 | loop fusion | flops 14680064 | bytes 58720704 | tf_op jit(solution)/shard_map/jit(_take)/select_n | solution.py:20
  709.6 321.5 %all_to_all.47 = bf16[8,1792,512]{2,1,0:T(8,128)(2,1)} all-to-all(bf16[8,1792,512]{2,1,0:T(8,128)(2,1)S(1)} %bitcast.80), channel_id=1, replica_groups=mesh['expert'=4,'unit'=8] {'unit'}, dimensions={0} | all-to-all | bytes 29360128 | tf_op jit(solution)/shard_map/all_to_all | solution.py:33
  1037.4 18.6 %copy.19 = bf16[1,1792,4096]{1,2,0:T(8,128)(2,1)} copy(bf16[1,1792,4096]{2,1,0:T(8,128)(2,1)} %param.8) | data formatting | bytes 29360128 | tf_op args[0]
  1056.0 18.8 %copy.23 = bf16[1,1792,4096]{1,2,0:T(8,128)(2,1)} copy(bf16[1,1792,4096]{2,1,0:T(8,128)(2,1)} %param.9) | data formatting | bytes 29360128 | tf_op args[1]
  1074.8 286.1 %all-gather.3.cloned.1.call-done = bf16[32,4,4096]{2,1,0:T(4,128)(2,1)} async-done(((bf16[1,4,4096]{2,1,0:T(4,128)(2,1)}), bf16[32,4,4096]{2,1,0:T(4,128)(2,1)}) %all-gather.3.cloned.1.call-update) | async-done | bytes 1048592 | tf_op jit(solution)/shard_map/all_gather | solution.py:38
  1362.2 16.8 %convert_bitcast_fusion.2 = f32[1792,8,512]{2,0,1:T(8,128)} fusion(bf16[8,1792,512]{2,1,0:T(8,128)(2,1)} %all_to_all.47), kind=kLoop, calls=%fused_computation.17 | loop fusion | flops 7340032 | bytes 44040192 | tf_op jit(solution)/shard_map/convert_element_type | solution.py:10
  1379.0 27.6 %copy.24 = f32[1792,8,512]{0,2,1:T(8,128)} copy(f32[1792,8,512]{2,0,1:T(8,128)} %convert_bitcast_fusion.2) | data formatting | bytes 58720256 | tf_op jit(solution)/shard_map/convert_element_type | solution.py:10
  1406.6 20.5 %fusion.9 = bf16[1792,4096]{0,1:T(8,128)(2,1)} fusion(bf16[1,1792,4096]{1,2,0:T(8,128)(2,1)} %copy.23, f32[1792,8,512]{0,2,1:T(8,128)} %copy.24), kind=kLoop, calls=%fused_computation.16 | loop fusion | flops 29360128 | bytes 58720256 | tf_op jit(solution)/shard_map/convert_element_type | solution.py:10
  1434.1 14.6 fusion.6
  1448.7 16.8 %convert_bitcast_fusion.3 = f32[1792,8,512]{2,0,1:T(8,128)} fusion(bf16[8,1792,512]{2,1,0:T(8,128)(2,1)} %all-to-all-done.1), kind=kLoop, calls=%fused_computation.18 | loop fusion | flops 7340032 | bytes 44040192 | tf_op jit(solution)/shard_map/convert_element_type | solution.py:10
  1465.4 27.6 %copy.22 = f32[1792,8,512]{0,2,1:T(8,128)} copy(f32[1792,8,512]{2,0,1:T(8,128)} %convert_bitcast_fusion.3) | data formatting | bytes 58720256 | tf_op jit(solution)/shard_map/convert_element_type | solution.py:10
  1493.1 20.5 %fusion.4 = bf16[1792,4096]{0,1:T(8,128)(2,1)} fusion(bf16[1,1792,4096]{1,2,0:T(8,128)(2,1)} %copy.19, f32[1792,8,512]{0,2,1:T(8,128)} %copy.22), kind=kLoop, calls=%fused_computation.11 | loop fusion | flops 29360128 | bytes 58720256 | tf_op jit(solution)/shard_map/convert_element_type | solution.py:10
  1520.5 14.6 fusion.1
  1535.1 20.1 %copy.28 = bf16[1,1792,4096]{2,1,0:T(8,128)(2,1)} copy(bf16[1,1792,4096]{1,2,0:T(8,128)(2,1)} %fusion.6) | data formatting | bytes 29360128
  1555.2 20.1 %copy.27 = bf16[1,1792,4096]{2,1,0:T(8,128)(2,1)} copy(bf16[1,1792,4096]{1,2,0:T(8,128)(2,1)} %fusion.1) | data formatting | bytes 29360128
  1575.3 7.3 fusion.22
  1582.6 8.3 fusion.11
  (26 shorter events, 52.7 us)
Async XLA Ops:
  25.8 325.3 %all-to-all-start = ((bf16[1792,8,512]{0,2,1:T(8,128)(2,1)}), bf16[1792,8,512]{0,2,1:T(8,128)(2,1)}, u32[]{:S(2)}, u32[]{:S(2)}) async-start(bf16[1792,8,512]{0,2,1:T(8,128)(2,1)} %bitcast.78), calls=%async_computation | async-start | bytes 29360128 | tf_op jit(solution)/shard_map/all_to_all | solution.py:23
  55.8 300.8 %copy-start.2 = (s32[1,448]{1,0:T(1,128)S(1)}, s32[1,448]{1,0:T(1,128)}, u32[]{:S(2)}) copy-start(s32[1,448]{1,0:T(1,128)} %param.12) | copy-start | bytes 5380
  351.1 322.6 %all-to-all-start.2 = ((bf16[8,1792,512]{2,1,0:T(8,128)(2,1)}), bf16[8,1792,512]{2,1,0:T(8,128)(2,1)}, u32[]{:S(2)}, u32[]{:S(2)}) async-start(bf16[8,1792,512]{2,1,0:T(8,128)(2,1)} %fusion.12), calls=%async_computation.2 | async-start | bytes 29360128 | tf_op jit(solution)/shard_map/all_to_all | solution.py:25
  1031.1 417.6 %all-to-all-start.1 = ((bf16[8,1792,512]{2,1,0:T(8,128)(2,1)}), bf16[8,1792,512]{2,1,0:T(8,128)(2,1)}, u32[]{:S(2)}, u32[]{:S(2)}) async-start(bf16[8,1792,512]{2,1,0:T(8,128)(2,1)} %bitcast.79), calls=%async_computation.1 | async-start | bytes 29360128 | tf_op jit(solution)/shard_map/all_to_all | solution.py:32
  1036.6 324.2 %all-gather.3.cloned.1.call-start = ((), (), s32[]{:S(2)}) async-start(), calls=%async_computation.4 | async-start | bytes 1081344 | tf_op jit(solution)/shard_map/all_gather | solution.py:38
  1406.6 27.5 %copy-start = (f32[1792,8,512]{0,2,1:T(8,128)S(1)}, f32[1792,8,512]{0,2,1:T(8,128)}, u32[]{:S(2)}) copy-start(f32[1792,8,512]{0,2,1:T(8,128)} %copy.24) | copy-start | bytes 88080384
  1493.1 27.5 %copy-start.1 = (f32[1792,8,512]{0,2,1:T(8,128)S(1)}, f32[1792,8,512]{0,2,1:T(8,128)}, u32[]{:S(2)}) copy-start(f32[1792,8,512]{0,2,1:T(8,128)} %copy.22) | copy-start | bytes 88080384
Sparse Core Ops, SparseCore 0:
  1040.4 320.3 all-gather.2
